TPU v7x, 32 devices: a whole 2x2x4 slice. The times are simulated.
32 devices in a mesh: dp: 8 (over y, x, core), branch: 4 (over z).
Axes of the slice: x: 2, y: 2, z: 4, core: 2. Of those that a mesh axis runs over, the one named last changes fastest.
Arguments:
- image_hidden: bfloat16 [4096, 1024], P('dp', 'branch'), may hold values from -8 to 8
- text_hidden: bfloat16 [4096, 768], P('dp', 'branch'), may hold values from -8 to 8
- image_proj: bfloat16 [1024, 768], replicated, may hold values from -0.1875 to 0.1875
- text_proj: bfloat16 [768, 768], replicated, may hold values from -0.21650635 to 0.21650635
- log_inverse_sharpness: float32 [1], replicated, may hold values from 4 to 5.9
- partner: int32 [4096], replicated, may hold values from 0 to 4095, each once
Outputs:
- loss: float32 [1], replicated
- grad_log_scale: float32 [1], replicated
- grad_image_hidden: bfloat16 [4096, 1024], P('dp', 'branch')
- grad_text_hidden: bfloat16 [4096, 768], P('dp', 'branch')
- grad_image_proj: float32 [1024, 768], P('branch')
- grad_text_proj: float32 [768, 768], P('branch')
Inputs may be any that keep to these rules, and one draw needn't show every extreme that they name: `partner`: each text index appears exactly once.
All inputs are finite; a program needn't handle non-finite values.
Results may differ from a plain program's by a relative error of at most 0.0029.
The roundings to bfloat16 on the way count: a program that leaves them out, or rounds other values in their place, can miss the bound.
Values may be sent and summed in bfloat16 or wider, within the bound.
A program may use at most 64 MiB of HBM per device.

v0:
```python
import jax
import jax.numpy as jnp
from jax import lax
from jax.sharding import PartitionSpec as P

NORM_EPSILON = 1e-06


def normalize(raw_rows):
    lengths = jnp.sqrt(jnp.sum(raw_rows * raw_rows, axis=1, keepdims=True) + NORM_EPSILON)
    unit_rows = raw_rows / lengths
    return (unit_rows, lengths, unit_rows.astype(jnp.bfloat16))


def unnormalize(upstream, unit_rows, lengths):
    radial = jnp.sum(upstream * unit_rows, axis=1, keepdims=True)
    return ((upstream - unit_rows * radial) / lengths).astype(jnp.bfloat16)


def per_device(image_hidden, text_hidden, image_proj, text_proj, log_inverse_sharpness, partner):
    branch_count = lax.axis_size("branch")
    data_count = lax.axis_size("dp")
    branch_pos = lax.axis_index("branch")
    data_pos = lax.axis_index("dp")
    group_rows = image_hidden.shape[0]
    own_rows = group_rows // branch_count
    image_cols = image_hidden.shape[1]
    text_cols = text_hidden.shape[1]
    image_slab = lax.dynamic_slice_in_dim(image_proj, branch_pos * image_cols, image_cols, 0)
    text_slab = lax.dynamic_slice_in_dim(text_proj, branch_pos * text_cols, text_cols, 0)
    image_local, text_local = (
        lax.all_to_all(image_hidden, "branch", split_axis=0, concat_axis=1, tiled=True),
        lax.all_to_all(text_hidden, "branch", split_axis=0, concat_axis=1, tiled=True),
    )
    image_raw = jnp.dot(image_local, image_proj, preferred_element_type=jnp.float32)
    text_raw = jnp.dot(text_local, text_proj, preferred_element_type=jnp.float32)
    image_unit, image_length, image_emb = normalize(image_raw)
    text_unit, text_length, caption_feature_entries = normalize(text_raw)
    normalized_exponent_divisor = jnp.exp(log_inverse_sharpness[0])
    column_count = own_rows * data_count
    total_pairs = group_rows * data_count
    denominator = 2.0 * total_pairs
    group_emb = lax.all_gather(image_emb, "branch", axis=0, tiled=True)
    row_partner = lax.dynamic_slice_in_dim(partner, data_pos * group_rows, group_rows, 0)

    def column_ident(positions):
        return (positions // own_rows * branch_count + branch_pos) * own_rows + positions % own_rows

    block_piece = lax.all_gather(caption_feature_entries, "dp", axis=0, tiled=True)
    row_peak = jnp.full((group_rows,), -jnp.inf, jnp.float32)
    row_mass = jnp.zeros((group_rows,), jnp.float32)
    piece_width = block_piece.shape[0]
    matching_cosine_scores = normalized_exponent_divisor * lax.dot_general(
        group_emb, block_piece, (((1,), (1,)), ((), ())), preferred_element_type=jnp.float32
    )
    logits_kept = matching_cosine_scores
    column_ids = column_ident(jnp.arange(piece_width, dtype=jnp.int32))
    matched = row_partner[:, None] == column_ids[None, :]
    positive = jnp.sum(jnp.where(matched, matching_cosine_scores, 0.0), axis=1)
    new_peak = jnp.max(matching_cosine_scores, axis=1)
    row_mass = row_mass * jnp.exp(row_peak - new_peak) + jnp.sum(
        jnp.exp(matching_cosine_scores - new_peak[:, None]), axis=1
    )
    piece_peak = jnp.max(matching_cosine_scores, axis=0)
    piece_mass = jnp.sum(jnp.exp(matching_cosine_scores - piece_peak[None, :]), axis=0)
    column_peak = piece_peak
    column_mass = piece_mass
    (
        retained_text_rows,
        matching_cosine_scores,
        row_peak,
        row_mass,
        positive,
        column_peak,
        column_mass,
    ) = (block_piece, logits_kept, new_peak, row_mass, positive, column_peak, column_mass)
    row_highest = lax.pmax(row_peak, "branch")
    row_mass, positive = lax.psum((row_mass * jnp.exp(row_peak - row_highest), positive), "branch")
    row_peak = row_highest
    column_highest = lax.pmax(column_peak, "dp")
    column_mass = lax.psum(column_mass * jnp.exp(column_peak - column_highest), "dp")
    column_peak = column_highest
    row_lse = row_peak + jnp.log(row_mass)
    col_lse = column_peak + jnp.log(column_mass)
    column_ids = column_ident(jnp.arange(column_count, dtype=jnp.int32))
    matched = (row_partner[:, None] == column_ids[None, :]).astype(jnp.float32)
    weights = (
        jnp.exp(matching_cosine_scores - row_lse[:, None])
        + jnp.exp(matching_cosine_scores - col_lse[None, :])
        - 2.0 * matched
    ) / denominator
    scale_part = jnp.sum(weights * matching_cosine_scores)
    reduced_width_parameters = weights.astype(jnp.bfloat16)
    picture_projection_matrix = lax.psum_scatter(
        normalized_exponent_divisor
        * jnp.dot(reduced_width_parameters, retained_text_rows, preferred_element_type=jnp.float32),
        "branch",
        scatter_dimension=0,
        tiled=True,
    )
    text_up = lax.psum_scatter(
        normalized_exponent_divisor
        * lax.dot_general(
            reduced_width_parameters,
            group_emb,
            (((0,), (0,)), ((), ())),
            preferred_element_type=jnp.float32,
        ),
        "dp",
        scatter_dimension=0,
        tiled=True,
    )
    image_down = unnormalize(picture_projection_matrix, image_unit, image_length)
    text_down = unnormalize(text_up, text_unit, text_length)
    image_gathered, text_gathered = (
        lax.all_gather(image_down, "branch", axis=0, tiled=True),
        lax.all_gather(text_down, "branch", axis=0, tiled=True),
    )
    grad_image_hidden = jnp.dot(
        image_gathered, image_slab.T, preferred_element_type=jnp.float32
    ).astype(jnp.bfloat16)
    grad_text_hidden = jnp.dot(
        text_gathered, text_slab.T, preferred_element_type=jnp.float32
    ).astype(jnp.bfloat16)
    image_weight = lax.dot_general(
        image_hidden, image_gathered, (((0,), (0,)), ((), ())), preferred_element_type=jnp.float32
    )
    text_weight = lax.dot_general(
        text_hidden, text_gathered, (((0,), (0,)), ((), ())), preferred_element_type=jnp.float32
    )
    grad_image_proj, grad_text_proj = lax.psum((image_weight, text_weight), "dp")
    own_row_terms = lax.dynamic_slice_in_dim(
        row_lse - 2.0 * positive, branch_pos * own_rows, own_rows, 0
    )
    own_col_terms = lax.dynamic_slice_in_dim(col_lse, data_pos * own_rows, own_rows, 0)
    loss_part = (jnp.sum(own_row_terms) + jnp.sum(own_col_terms)) / denominator
    loss_total, scale_total = lax.psum((loss_part, scale_part), ("dp", "branch"))
    return (
        loss_total.reshape(1),
        scale_total.reshape(1),
        grad_image_hidden,
        grad_text_hidden,
        grad_image_proj,
        grad_text_proj,
    )


def solution(mesh):
    placed = (P("dp", "branch"), P("dp", "branch"), P(), P(), P(), P())
    return jax.shard_map(
        per_device,
        mesh=mesh,
        in_specs=placed,
        out_specs=(
            P(),
            P(),
            P("dp", "branch"),
            P("dp", "branch"),
            P("branch", None),
            P("branch", None),
        ),
        check_vma=False,
    )
```

profile of v0, /device:TPU:0, one launch (start us, length us, event | category | flops | bytes accessed | tf_op | source)
XLA Modules:
  0.0 283.1 jit_solution(11487178637805667783)
XLA Ops:
  7.2 0.0 copy-start
  7.2 0.0 all-gather.2.cloned.1.call-start
  7.2 1.1 copy_bitcast_fusion
  8.3 13.6 %all_to_all.38 = bf16[4,128,192]{1,2,0:T(8,128)(2,1)S(1)} all-to-all(bf16[4,128,192]{1,2,0:T(8,128)(2,1)S(1)} %copy_bitcast_fusion), channel_id=1, replica_groups=mesh['dp'=8,'branch'=4] {'branch'}, dimensions={0} | all-to-all | bytes 393216 | tf_op jit(solution)/shard_map/all_to_all | solution.py:33
  21.9 1.7 multiply_reduce_fusion.3
  23.7 0.8 fusion.20
  24.4 0.0 all-gather.2.cloned.1.call-update
  24.5 3.4 %all-to-all-start = ((bf16[4,128,256]{2,1,0:T(8,128)(2,1)}), bf16[4,128,256]{2,1,0:T(8,128)(2,1)S(1)}, u32[]{:S(2)}, u32[]{:S(2)}) async-start(bf16[4,128,256]{2,1,0:T(8,128)(2,1)} %bitcast.1), calls=%async_computation | async-start | bytes 524288 | tf_op jit(solution)/shard_map/all_to_all | solution.py:32
  27.9 0.0 reduce-scatter.3.cloned.1.call-start
  28.6 0.8 dynamic_slice.15
  29.4 6.6 %all-to-all-done = bf16[4,128,256]{2,1,0:T(8,128)(2,1)S(1)} async-done(((bf16[4,128,256]{2,1,0:T(8,128)(2,1)}), bf16[4,128,256]{2,1,0:T(8,128)(2,1)S(1)}, u32[]{:S(2)}, u32[]{:S(2)}) %all-to-all-start) | async-done | bytes 262176 | tf_op jit(solution)/shard_map/all_to_all | solution.py:32
  36.0 0.2 copy.17
  36.2 0.5 multiply_reduce_fusion.4
  36.7 0.1 fusion.19
  36.8 17.6 %all_gather.12 = bf16[512,768]{1,0:T(8,128)(2,1)S(1)} all-gather(bf16[128,768]{1,0:T(8,128)(2,1)S(1)} %fusion.19), channel_id=1, replica_groups=mesh['dp'=8,'branch'=4] {'branch'}, dimensions={0}, use_global_device_ids=true | all-gather | bytes 983040 | tf_op jit(solution)/shard_map/all_gather | solution.py:43
  54.4 3.8 %fusion.23 = (f32[1024]{0:T(1024)S(1)}, f32[512]{0:T(512)S(1)}, f32[512,1024]{1,0:T(8,128)}) fusion(bf16[512,768]{1,0:T(8,128)(2,1)S(1)} %all_gather.12, bf16[1024,768]{1,0:T(8,128)(2,1)} %all-gather.2.cloned.1.call-done, f32[]{:T(128)} %bitcast), kind=kOutput, calls=%fused_computation.55 | convolution fusion | flops 806877696 | bytes 4462596 | tf_op jit(solution)/shard_map/dot_general | solution.py:53
  58.2 10.3 %pmax.14 = f32[512]{0:T(512)S(1)} all-reduce(f32[512]{0:T(512)S(1)} %get-tuple-element.35), channel_id=1, replica_groups=mesh['dp'=8,'branch'=4] {'branch'}, use_global_device_ids=true, to_apply=%region_3.4 | all-reduce | flops 512 | bytes 4096 | tf_op jit(solution)/shard_map/pmax | solution.py:77
  68.5 11.8 %pmax.15 = f32[1024]{0:T(1024)S(1)} all-reduce(f32[1024]{0:T(1024)S(1)} %get-tuple-element.34), channel_id=1, replica_groups=mesh['dp'=8,'branch'=4] {'dp'}, use_global_device_ids=true, to_apply=%region_10.11 | all-reduce | flops 1024 | bytes 8192 | tf_op jit(solution)/shard_map/pmax | solution.py:80
  80.3 2.3 exponential_reduce_fusion
  82.7 11.9 %psum.51 = f32[1024]{0:T(1024)S(1)} all-reduce(f32[1024]{0:T(1024)S(1)} %exponential_multiply_fusion), channel_id=1, replica_groups=mesh['dp'=8,'branch'=4] {'dp'}, use_global_device_ids=true, to_apply=%region_12.13 | all-reduce | flops 1024 | bytes 8192 | tf_op jit(solution)/shard_map/psum | solution.py:81
  94.6 8.4 %psum.49 = f32[512]{0:T(512)S(1)} all-reduce(f32[512]{0:T(512)S(1)} %exponential_multiply_fusion.1), channel_id=1, replica_groups=mesh['dp'=8,'branch'=4] {'branch'}, use_global_device_ids=true, to_apply=%region_5.6 | all-reduce | flops 512 | bytes 4096 | tf_op jit(solution)/shard_map/psum | solution.py:78
  103.0 4.8 %convolution_multiply_fusion.2 = f32[512,768]{1,0:T(8,128)} fusion(bf16[1024,768]{1,0:T(8,128)(2,1)} %all-gather.2.cloned.1.call-done, f32[]{:T(128)} %bitcast, f32[512,1024]{1,0:T(8,128)} %get-tuple-element.44, f32[1024]{0:T(1024)S(1)} %log_add_fusion, f32[512]{0:T(512)S(1)} %log_add_fusion.1, s32[1024]{0:T(1024)S(1)} %fusion.15, s32[512]{0:T(512)S(1)} %dynamic_slice.15), kind=kOutput, calls=%fused_computation.11 | convolution fusion | flops 809893888 | bytes 5255172 | tf_op jit(solution)/shard_map/dot_general | solution.py:96
  107.8 0.0 reduce-scatter.3.cloned.1.call-update
  107.8 0.0 reduce-scatter.5.cloned.1.call-start
  107.9 4.8 %convolution_multiply_fusion = f32[1024,768]{1,0:T(8,128)} fusion(bf16[512,768]{1,0:T(8,128)(2,1)S(1)} %all_gather.12, f32[]{:T(128)} %bitcast, f32[512,1024]{1,0:T(8,128)} %get-tuple-element.44, f32[1024]{0:T(1024)S(1)} %log_add_fusion, f32[512]{0:T(512)S(1)} %log_add_fusion.1, s32[1024]{0:T(1024)S(1)} %fusion.15, s32[512]{0:T(512)S(1)} %dynamic_slice.15), kind=kOutput, calls=%fused_computation.9 | convolution fusion | flops 810287104 | bytes 6041604 | tf_op jit(solution)/shard_map/dot_general | solution.py:103
  112.7 0.0 reduce-scatter.5.cloned.1.call-update
  112.8 0.0 all-reduce.4.cloned.1.call-start
  112.8 0.7 dynamic-slice_reduce_fusion
  113.5 3.6 %multiply_reduce_fusion = (f32[]{:T(128)}, f32[512]{0:T(512)S(1)}) fusion(f32[512,1024]{1,0:T(8,128)} %get-tuple-element.44, f32[1024]{0:T(1024)S(1)} %log_add_fusion, f32[512]{0:T(512)S(1)} %log_add_fusion.1, s32[1024]{0:T(1024)S(1)} %fusion.15, s32[512]{0:T(512)S(1)} %dynamic_slice.15), kind=kLoop, calls=%fused_computation.5 | loop fusion | flops 5766655 | bytes 2111492 | tf_op jit(solution)/shard_map/reduce_sum | solution.py:92
  117.1 11.2 %psum.50 = f32[512]{0:T(512)S(1)} all-reduce(f32[512]{0:T(512)S(1)} %get-tuple-element.31), channel_id=1, replica_groups=mesh['dp'=8,'branch'=4] {'branch'}, use_global_device_ids=true, to_apply=%region_7.8 | all-reduce | flops 512 | bytes 4096 | tf_op jit(solution)/shard_map/psum | solution.py:78
  128.3 14.0 %reduce-scatter.3.cloned.1.call-done = f32[128,768]{1,0:T(8,128)} async-done(((f32[512,768]{1,0:T(8,128)}), f32[128,768]{1,0:T(8,128)}) %reduce-scatter.3.cloned.1.call-update) | async-done | bytes 393232 | tf_op jit(solution)/shard_map/reduce_scatter | solution.py:94
  142.3 1.2 multiply_reduce_fusion.2
  143.5 1.1 divide_convert_fusion.1
  144.6 17.9 %all_gather.14 = bf16[512,768]{1,0:T(8,128)(2,1)S(1)} all-gather(bf16[128,768]{1,0:T(8,128)(2,1)S(1)} %divide_convert_fusion.1), channel_id=1, replica_groups=mesh['dp'=8,'branch'=4] {'branch'}, dimensions={0}, use_global_device_ids=true | all-gather | bytes 983040 | tf_op jit(solution)/shard_map/all_gather | solution.py:116
  162.5 2.2 convolution_bitcast_fusion
  164.8 25.9 %reduce-scatter.5.cloned.1.call-done = f32[128,768]{1,0:T(8,128)} async-done(((f32[1024,768]{1,0:T(8,128)}), f32[128,768]{1,0:T(8,128)}) %reduce-scatter.5.cloned.1.call-update) | async-done | bytes 393232 | tf_op jit(solution)/shard_map/reduce_scatter | solution.py:101
  190.7 1.2 multiply_reduce_fusion.1
  191.8 1.1 divide_convert_fusion
  193.0 19.6 %all_gather.15 = bf16[512,768]{1,0:T(8,128)(2,1)S(1)} all-gather(bf16[128,768]{1,0:T(8,128)(2,1)S(1)} %divide_convert_fusion), channel_id=1, replica_groups=mesh['dp'=8,'branch'=4] {'branch'}, dimensions={0}, use_global_device_ids=true | all-gather | bytes 983040 | tf_op jit(solution)/shard_map/all_gather | solution.py:117
  212.5 2.1 convolution_bitcast_fusion.1
  214.6 0.0 all-reduce.4.cloned.1.call-update
  214.6 0.7 dynamic-slice_reduce_fusion.1
  216.6 38.5 %all-reduce = (f32[1]{0:T(128)}, f32[1]{0:T(128)}) all-reduce(f32[1]{0:T(128)} %bitcast.6, f32[1]{0:T(128)} %bitcast.7), channel_id=1, replica_groups=mesh['dp'=8,'branch'=4] {'dp','branch'}, use_global_device_ids=true, to_apply=%region_14.15 | all-reduce | flops 2 | bytes 16 | tf_op jit(solution)/shard_map/psum | solution.py:137
  255.1 1.1 convolution_convert_fusion
  256.2 2.0 convolution_convert_fusion.1
  258.3 14.1 %all-reduce.4.cloned.1.call-done = (f32[256,768]{0,1:T(8,128)}, f32[192,768]{1,0:T(8,128)}) async-done(((f32[256,768]{0,1:T(8,128)}, f32[192,768]{1,0:T(8,128)}), (f32[256,768]{0,1:T(8,128)}, f32[192,768]{1,0:T(8,128)})) %all-reduce.4.cloned.1.call-update) | async-done | bytes 1376272 | tf_op jit(solution)/shard_map/psum | solution.py:131
  272.3 2.3 copy.19
  274.6 1.9 copy.25
  (10 shorter events, 0.1 us)
Async XLA Ops:
  7.2 29.0 %copy-start = (bf16[1024,768]{1,0:T(8,128)(2,1)S(1)}, bf16[1024,768]{1,0:T(8,128)(2,1)}, u32[]{:S(2)}) copy-start(bf16[1024,768]{1,0:T(8,128)(2,1)} %param.8) | copy-start | bytes 4718596
  7.2 47.2 %all-gather.2.cloned.1.call-start = ((), (), s32[]{:S(2)}) async-start(), calls=%async_computation.4 | async-start | bytes 1769472 | tf_op jit(solution)/shard_map/all_gather | solution.py:49
  24.5 11.6 %all-to-all-start = ((bf16[4,128,256]{2,1,0:T(8,128)(2,1)}), bf16[4,128,256]{2,1,0:T(8,128)(2,1)S(1)}, u32[]{:S(2)}, u32[]{:S(2)}) async-start(bf16[4,128,256]{2,1,0:T(8,128)(2,1)} %bitcast.1), calls=%async_computation | async-start | bytes 524288 | tf_op jit(solution)/shard_map/all_to_all | solution.py:32
  27.9 114.4 %reduce-scatter.3.cloned.1.call-start = ((), (), s32[]{:S(2)}) async-start(), calls=%async_computation.5 | async-start | bytes 1966080 | tf_op jit(solution)/shard_map/reduce_scatter | solution.py:94
  107.8 82.8 %reduce-scatter.5.cloned.1.call-start = ((), (), s32[]{:S(2)}) async-start(), calls=%async_computation.6 | async-start | bytes 3538944 | tf_op jit(solution)/shard_map/reduce_scatter | solution.py:101
  112.8 159.6 %all-reduce.4.cloned.1.call-start = ((), (), s32[]{:S(2)}) async-start(), calls=%async_computation.7 | async-start | bytes 2752512 | tf_op jit(solution)/shard_map/psum | solution.py:131
Sparse Core Ops, SparseCore 0:
  24.6 24.6 all-gather.1
  108.0 34.2 reduce-scatter.2
  145.7 44.9 reduce-scatter.4
  214.8 57.5 all-reduce.3
where the time goes:
time: 284 us; the launch traced here: 283 us
  blocking collectives  161 us (57%)
  waiting for transfers between devices  60.6 us (21%)
  matrix products  23.1 us (8%)
  between operations  15.9 us (6%)
  other arithmetic  12.9 us (5%)
  local copies, waits for them, and re-layouts  6.21 us (2%)
  starting transfers between devices  3.58 us (1%)
    psum x1, blocking collectives, per_device(): lax.psum((loss_part, scale_part), ('dp', 'branch'))  38.5 us
    reduce_scatter x1, waiting for transfers between devices, per_device(): lax.psum_scatter(normalized_exponent_divisor * lax.dot_general(reduced_wi...  25.9 us
    all_gather x1, blocking collectives, per_device(): lax.all_gather(text_down, 'branch', axis=0, tiled=True)  19.6 us
    psum x2, blocking collectives, per_device(): lax.psum((row_mass * jnp.exp(row_peak - row_highest), positive), 'branch')  19.6 us
    all_gather x1, blocking collectives, per_device(): lax.all_gather(image_down, 'branch', axis=0, tiled=True)  17.9 us
    all_gather x1, blocking collectives, per_device(): group_emb = lax.all_gather(image_emb, 'branch', axis=0, tiled=True)  17.6 us
    psum x1, waiting for transfers between devices, per_device(): lax.psum((image_weight, text_weight), 'dp')  14.1 us
    reduce_scatter x1, waiting for transfers between devices, per_device(): lax.psum_scatter(normalized_exponent_divisor * jnp.dot(reduced_width_para...  14 us
  transfers between devices with their start and end apart: 5, of which 4 were waited for; matrix products, arithmetic and copies ran while one was open for 7% of the time, Pallas kernels for 0%

commit v1 on v0

--- a/solution.py
+++ b/solution.py
@@ -1,9 +1,19 @@
+import functools
 import jax
 import jax.numpy as jnp
 from jax import lax
 from jax.sharding import PartitionSpec as P
 
 NORM_EPSILON = 1e-06
+
+
+def end_the_widths(arr_in, lane_axis, mesh_ax):
+    for ii in (lane_axis, mesh_ax):
+        arr_in = lax.psum(arr_in, axis_name=ii)
+    return arr_in
+
+
+refer_the_indices = functools.partial(end_the_widths, lane_axis="dp", mesh_ax="branch")
 
 
 def normalize(raw_rows):
@@ -134,7 +144,7 @@
     )
     own_col_terms = lax.dynamic_slice_in_dim(col_lse, data_pos * own_rows, own_rows, 0)
     loss_part = (jnp.sum(own_row_terms) + jnp.sum(own_col_terms)) / denominator
-    loss_total, scale_total = lax.psum((loss_part, scale_part), ("dp", "branch"))
+    loss_total, scale_total = refer_the_indices((loss_part, scale_part))
     return (
         loss_total.reshape(1),
         scale_total.reshape(1),

time: 284 us -> 284 us (level)
  blocking collectives: 161 us -> 146 us
  waiting for transfers between devices: 60.6 us -> 75.2 us
    psum x1 -> x2, blocking collectives: 38.5 us -> 23.4 us  [end_the_widths(): arr_in = lax.psum(arr_in, axis_name=ii)]
    psum x1, waiting for transfers between devices: 14.1 us -> 28.7 us  [per_device(): lax.psum((image_weight, text_weight), 'dp')]
where the time goes in v1:
time: 284 us; the launch traced here: 283 us
  blocking collectives  146 us (51%)
  waiting for transfers between devices  75.2 us (26%)
  matrix products  23.1 us (8%)
  between operations  15.9 us (6%)
  other arithmetic  12.9 us (5%)
  local copies, waits for them, and re-layouts  6.21 us (2%)
  starting transfers between devices  3.58 us (1%)
    psum x1, waiting for transfers between devices, per_device(): lax.psum((image_weight, text_weight), 'dp')  28.7 us
    reduce_scatter x1, waiting for transfers between devices, per_device(): lax.psum_scatter(normalized_exponent_divisor * lax.dot_general(reduced_wi...  25.9 us
    psum x2, blocking collectives, end_the_widths(): arr_in = lax.psum(arr_in, axis_name=ii)  23.4 us
    all_gather x1, blocking collectives, per_device(): lax.all_gather(text_down, 'branch', axis=0, tiled=True)  19.6 us
    psum x2, blocking collectives, per_device(): lax.psum((row_mass * jnp.exp(row_peak - row_highest), positive), 'branch')  19.6 us
    all_gather x1, blocking collectives, per_device(): lax.all_gather(image_down, 'branch', axis=0, tiled=True)  17.9 us
    all_gather x1, blocking collectives, per_device(): group_emb = lax.all_gather(image_emb, 'branch', axis=0, tiled=True)  17.6 us
    reduce_scatter x1, waiting for transfers between devices, per_device(): lax.psum_scatter(normalized_exponent_divisor * jnp.dot(reduced_width_para...  14 us
  transfers between devices with their start and end apart: 5, of which 4 were waited for; matrix products, arithmetic and copies ran while one was open for 7% of the time, Pallas kernels for 0%

profile of v1, /device:TPU:0, one launch (start us, length us, event | category | flops | bytes accessed | tf_op | source)
XLA Modules:
  0.0 282.5 jit_solution(16634384593390737706)
XLA Ops:
  7.2 0.0 all-gather.2.cloned.1.call-start
  7.2 1.1 copy_bitcast_fusion
  8.3 13.6 %all_to_all.38 = bf16[4,128,192]{1,2,0:T(8,128)(2,1)S(1)} all-to-all(bf16[4,128,192]{1,2,0:T(8,128)(2,1)S(1)} %copy_bitcast_fusion), channel_id=1, replica_groups=mesh['dp'=8,'branch'=4] {'branch'}, dimensions={0} | all-to-all | bytes 393216 | tf_op jit(solution)/shard_map/all_to_all | solution.py:43
  21.9 1.7 multiply_reduce_fusion.3
  23.7 0.8 fusion.20
  24.4 0.0 all-gather.2.cloned.1.call-update
  24.5 3.4 %all-to-all-start = ((bf16[4,128,256]{2,1,0:T(8,128)(2,1)}), bf16[4,128,256]{2,1,0:T(8,128)(2,1)S(1)}, u32[]{:S(2)}, u32[]{:S(2)}) async-start(bf16[4,128,256]{2,1,0:T(8,128)(2,1)} %bitcast.1), calls=%async_computation | async-start | bytes 524288 | tf_op jit(solution)/shard_map/all_to_all | solution.py:42
  27.9 0.0 reduce-scatter.3.cloned.1.call-start
  28.6 0.8 dynamic_slice.15
  29.4 6.6 %all-to-all-done = bf16[4,128,256]{2,1,0:T(8,128)(2,1)S(1)} async-done(((bf16[4,128,256]{2,1,0:T(8,128)(2,1)}), bf16[4,128,256]{2,1,0:T(8,128)(2,1)S(1)}, u32[]{:S(2)}, u32[]{:S(2)}) %all-to-all-start) | async-done | bytes 262176 | tf_op jit(solution)/shard_map/all_to_all | solution.py:42
  36.0 0.2 copy.17
  36.2 0.5 multiply_reduce_fusion.4
  36.7 0.1 fusion.19
  36.8 17.6 %all_gather.12 = bf16[512,768]{1,0:T(8,128)(2,1)S(1)} all-gather(bf16[128,768]{1,0:T(8,128)(2,1)S(1)} %fusion.19), channel_id=1, replica_groups=mesh['dp'=8,'branch'=4] {'branch'}, dimensions={0}, use_global_device_ids=true | all-gather | bytes 983040 | tf_op jit(solution)/shard_map/all_gather | solution.py:53
  54.4 3.8 %fusion.23 = (f32[1024]{0:T(1024)S(1)}, f32[512]{0:T(512)S(1)}, f32[512,1024]{1,0:T(8,128)}) fusion(bf16[512,768]{1,0:T(8,128)(2,1)S(1)} %all_gather.12, bf16[1024,768]{1,0:T(8,128)(2,1)} %all-gather.2.cloned.1.call-done, f32[]{:T(128)} %bitcast), kind=kOutput, calls=%fused_computation.55 | convolution fusion | flops 806877696 | bytes 4462596 | tf_op jit(solution)/shard_map/dot_general | solution.py:63
  58.2 10.3 %pmax.14 = f32[512]{0:T(512)S(1)} all-reduce(f32[512]{0:T(512)S(1)} %get-tuple-element.35), channel_id=1, replica_groups=mesh['dp'=8,'branch'=4] {'branch'}, use_global_device_ids=true, to_apply=%region_3.4 | all-reduce | flops 512 | bytes 4096 | tf_op jit(solution)/shard_map/pmax | solution.py:87
  68.5 11.8 %pmax.15 = f32[1024]{0:T(1024)S(1)} all-reduce(f32[1024]{0:T(1024)S(1)} %get-tuple-element.34), channel_id=1, replica_groups=mesh['dp'=8,'branch'=4] {'dp'}, use_global_device_ids=true, to_apply=%region_10.11 | all-reduce | flops 1024 | bytes 8192 | tf_op jit(solution)/shard_map/pmax | solution.py:90
  80.3 2.3 exponential_reduce_fusion
  82.7 11.9 %psum.65 = f32[1024]{0:T(1024)S(1)} all-reduce(f32[1024]{0:T(1024)S(1)} %exponential_multiply_fusion), channel_id=1, replica_groups=mesh['dp'=8,'branch'=4] {'dp'}, use_global_device_ids=true, to_apply=%region_12.13 | all-reduce | flops 1024 | bytes 8192 | tf_op jit(solution)/shard_map/psum | solution.py:91
  94.6 8.4 %psum.63 = f32[512]{0:T(512)S(1)} all-reduce(f32[512]{0:T(512)S(1)} %exponential_multiply_fusion.1), channel_id=1, replica_groups=mesh['dp'=8,'branch'=4] {'branch'}, use_global_device_ids=true, to_apply=%region_5.6 | all-reduce | flops 512 | bytes 4096 | tf_op jit(solution)/shard_map/psum | solution.py:88
  103.0 4.8 %convolution_multiply_fusion.2 = f32[512,768]{1,0:T(8,128)} fusion(bf16[1024,768]{1,0:T(8,128)(2,1)} %all-gather.2.cloned.1.call-done, f32[]{:T(128)} %bitcast, f32[512,1024]{1,0:T(8,128)} %get-tuple-element.46, f32[1024]{0:T(1024)S(1)} %log_add_fusion, f32[512]{0:T(512)S(1)} %log_add_fusion.1, s32[1024]{0:T(1024)S(1)} %fusion.15, s32[512]{0:T(512)S(1)} %dynamic_slice.15), kind=kOutput, calls=%fused_computation.11 | convolution fusion | flops 809893888 | bytes 5255172 | tf_op jit(solution)/shard_map/dot_general | solution.py:106
  107.8 0.0 reduce-scatter.3.cloned.1.call-update
  107.8 0.0 reduce-scatter.5.cloned.1.call-start
  107.9 4.8 %convolution_multiply_fusion = f32[1024,768]{1,0:T(8,128)} fusion(bf16[512,768]{1,0:T(8,128)(2,1)S(1)} %all_gather.12, f32[]{:T(128)} %bitcast, f32[512,1024]{1,0:T(8,128)} %get-tuple-element.46, f32[1024]{0:T(1024)S(1)} %log_add_fusion, f32[512]{0:T(512)S(1)} %log_add_fusion.1, s32[1024]{0:T(1024)S(1)} %fusion.15, s32[512]{0:T(512)S(1)} %dynamic_slice.15), kind=kOutput, calls=%fused_computation.9 | convolution fusion | flops 810287104 | bytes 6041604 | tf_op jit(solution)/shard_map/dot_general | solution.py:113
  112.7 0.0 reduce-scatter.5.cloned.1.call-update
  112.8 0.0 all-reduce.5.cloned.1.call-start
  112.8 0.7 dynamic-slice_reduce_fusion
  113.5 3.6 %multiply_reduce_fusion = (f32[]{:T(128)}, f32[512]{0:T(512)S(1)}) fusion(f32[512,1024]{1,0:T(8,128)} %get-tuple-element.46, f32[1024]{0:T(1024)S(1)} %log_add_fusion, f32[512]{0:T(512)S(1)} %log_add_fusion.1, s32[1024]{0:T(1024)S(1)} %fusion.15, s32[512]{0:T(512)S(1)} %dynamic_slice.15), kind=kLoop, calls=%fused_computation.5 | loop fusion | flops 5766655 | bytes 2111492 | tf_op jit(solution)/shard_map/reduce_sum | solution.py:102
  117.1 11.2 %psum.64 = f32[512]{0:T(512)S(1)} all-reduce(f32[512]{0:T(512)S(1)} %get-tuple-element.31), channel_id=1, replica_groups=mesh['dp'=8,'branch'=4] {'branch'}, use_global_device_ids=true, to_apply=%region_7.8 | all-reduce | flops 512 | bytes 4096 | tf_op jit(solution)/shard_map/psum | solution.py:88
  128.3 14.0 %reduce-scatter.3.cloned.1.call-done = f32[128,768]{1,0:T(8,128)} async-done(((f32[512,768]{1,0:T(8,128)}), f32[128,768]{1,0:T(8,128)}) %reduce-scatter.3.cloned.1.call-update) | async-done | bytes 393232 | tf_op jit(solution)/shard_map/reduce_scatter | solution.py:104
  142.3 1.2 multiply_reduce_fusion.2
  143.5 1.1 divide_convert_fusion.1
  144.6 17.9 %all_gather.14 = bf16[512,768]{1,0:T(8,128)(2,1)S(1)} all-gather(bf16[128,768]{1,0:T(8,128)(2,1)S(1)} %divide_convert_fusion.1), channel_id=1, replica_groups=mesh['dp'=8,'branch'=4] {'branch'}, dimensions={0}, use_global_device_ids=true | all-gather | bytes 983040 | tf_op jit(solution)/shard_map/all_gather | solution.py:126
  162.5 2.2 convolution_bitcast_fusion
  164.8 25.9 %reduce-scatter.5.cloned.1.call-done = f32[128,768]{1,0:T(8,128)} async-done(((f32[1024,768]{1,0:T(8,128)}), f32[128,768]{1,0:T(8,128)}) %reduce-scatter.5.cloned.1.call-update) | async-done | bytes 393232 | tf_op jit(solution)/shard_map/reduce_scatter | solution.py:111
  190.7 1.2 multiply_reduce_fusion.1
  191.8 1.1 divide_convert_fusion
  193.0 19.6 %all_gather.15 = bf16[512,768]{1,0:T(8,128)(2,1)S(1)} all-gather(bf16[128,768]{1,0:T(8,128)(2,1)S(1)} %divide_convert_fusion), channel_id=1, replica_groups=mesh['dp'=8,'branch'=4] {'branch'}, dimensions={0}, use_global_device_ids=true | all-gather | bytes 983040 | tf_op jit(solution)/shard_map/all_gather | solution.py:127
  212.5 2.1 convolution_bitcast_fusion.1
  214.6 0.0 all-reduce.5.cloned.1.call-update
  214.6 0.7 dynamic-slice_reduce_fusion.1
  216.6 12.8 %all-reduce = (f32[]{:T(128)}, f32[]{:T(128)}) all-reduce(f32[]{:T(128)S(6)} %div.53, f32[]{:T(128)} %get-tuple-element.30), channel_id=1, replica_groups=mesh['dp'=8,'branch'=4] {'dp'}, use_global_device_ids=true, to_apply=%region_14.15 | all-reduce | flops 2 | bytes 16 | tf_op jit(solution)/shard_map/psum | solution.py:12
  229.4 10.6 %all-reduce.2 = (f32[1]{0:T(128)}, f32[1]{0:T(128)}) all-reduce(f32[1]{0:T(128)} %bitcast.6, f32[1]{0:T(128)} %bitcast.7), channel_id=1, replica_groups=mesh['dp'=8,'branch'=4] {'branch'}, use_global_device_ids=true, to_apply=%region_15.16 | all-reduce | flops 2 | bytes 16 | tf_op jit(solution)/shard_map/psum | solution.py:12
  240.0 1.1 convolution_convert_fusion
  241.1 2.0 convolution_convert_fusion.1
  243.2 28.7 %all-reduce.5.cloned.1.call-done = (f32[256,768]{0,1:T(8,128)}, f32[192,768]{1,0:T(8,128)}) async-done(((f32[256,768]{0,1:T(8,128)}, f32[192,768]{1,0:T(8,128)}), (f32[256,768]{0,1:T(8,128)}, f32[192,768]{1,0:T(8,128)})) %all-reduce.5.cloned.1.call-update) | async-done | bytes 1376272 | tf_op jit(solution)/shard_map/psum | solution.py:141
  271.8 2.3 copy.19
  274.1 1.9 copy.25
  (11 shorter events, 0.1 us)
Async XLA Ops:
  7.2 29.0 %copy-start = (bf16[1024,768]{1,0:T(8,128)(2,1)S(1)}, bf16[1024,768]{1,0:T(8,128)(2,1)}, u32[]{:S(2)}) copy-start(bf16[1024,768]{1,0:T(8,128)(2,1)} %param.8) | copy-start | bytes 4718596
  7.2 47.2 %all-gather.2.cloned.1.call-start = ((), (), s32[]{:S(2)}) async-start(), calls=%async_computation.4 | async-start | bytes 1769472 | tf_op jit(solution)/shard_map/all_gather | solution.py:59
  24.5 11.6 %all-to-all-start = ((bf16[4,128,256]{2,1,0:T(8,128)(2,1)}), bf16[4,128,256]{2,1,0:T(8,128)(2,1)S(1)}, u32[]{:S(2)}, u32[]{:S(2)}) async-start(bf16[4,128,256]{2,1,0:T(8,128)(2,1)} %bitcast.1), calls=%async_computation | async-start | bytes 524288 | tf_op jit(solution)/shard_map/all_to_all | solution.py:42
  27.9 114.4 %reduce-scatter.3.cloned.1.call-start = ((), (), s32[]{:S(2)}) async-start(), calls=%async_computation.5 | async-start | bytes 1966080 | tf_op jit(solution)/shard_map/reduce_scatter | solution.py:104
  107.8 82.8 %reduce-scatter.5.cloned.1.call-start = ((), (), s32[]{:S(2)}) async-start(), calls=%async_computation.6 | async-start | bytes 3538944 | tf_op jit(solution)/shard_map/reduce_scatter | solution.py:111
  112.8 159.1 %all-reduce.5.cloned.1.call-start = ((), (), s32[]{:S(2)}) async-start(), calls=%async_computation.7 | async-start | bytes 2752512 | tf_op jit(solution)/shard_map/psum | solution.py:141
Sparse Core Ops, SparseCore 0:
  24.6 24.6 all-gather.1
  108.0 34.2 reduce-scatter.2
  145.7 44.9 reduce-scatter.4
  214.8 57.0 all-reduce.4
